TPU v7x, 256 devices: a whole 4x4x8 slice. The times are simulated.
256 devices in a mesh: row: 128 (over y, x, z), col: 2 (over core).
Axes of the slice: x: 4, y: 4, z: 8, core: 2. Of those that a mesh axis runs over, the one named last changes fastest.
Arguments:
- features: float32 [64, 32768], P(None, ('row', 'col')), may hold values from -12 to 12
- initial: float32 [32768], P(('row', 'col')), may hold values from 0.1 to 90, as said below
Outputs:
- dist: float32 [32768], P(('row', 'col'))
- residuals: float32 [2], replicated
Inputs may be any that keep to these rules, and one draw needn't show every extreme that they name: `initial`: positive starting weights of the policies.
All inputs are finite; a program needn't handle non-finite values.
Results may differ from a plain program's by a relative error of at most 0.0003.
Values sent between devices are 32-bit elements; how exact they have to be, the bound alone decides.
No kernel may reach another device: no remote copies, remote signals or barrier semaphores. Data moves between devices by JAX's collectives and lax.ppermute only.
A program may use at most 64 MiB of HBM per device.

v0:
```python
import functools
import math
import jax
import jax.numpy as jnp
from jax import lax
from jax.sharding import Mesh
from jax.sharding import PartitionSpec as P

NPOL = 32768
ITERS = 2
ROW_COL = ("row_0", "row_1", "row_2", "col")
ROW = ("row_0", "row_1", "row_2")
intensity = 0.25
column_block = 2048


def in_order(blocks, dim):
    lengths = list(blocks.shape[1:])
    lengths[dim] *= blocks.shape[0]
    return jnp.moveaxis(blocks, 0, dim).reshape(lengths)


def copy_for_each(array, axis):
    copies = jnp.broadcast_to(array, (lax.axis_size(axis), *array.shape))
    return lax.all_to_all(copies, axis, split_axis=0, concat_axis=0, tiled=True)


def gathered_copies(array, axis, dim):
    return in_order(copy_for_each(array, axis), dim)


def one_axis_at_a_time(array, axes):
    return functools.reduce(lax.psum, axes, array)


def all_blocks(array, axes, turns):
    blocks = array[None]
    for k in turns:
        blocks = lax.all_gather(blocks, axes[k], axis=0, tiled=True)
    block = [lax.axis_size(axes[k]) for k in reversed(turns)]
    blocks = blocks.reshape(*block, *array.shape)
    turned = sorted(range(len(turns)), key=lambda place: turns[len(turns) - 1 - place])
    return blocks.transpose(*turned, *range(len(turns), blocks.ndim)).reshape(-1, *array.shape)


def gathered_by_axis(array, axes, turns, dim):
    return in_order(all_blocks(array, axes, turns), dim)


def cut_along(array, dim, count):
    lengths = array.shape
    blocks = array.reshape(*lengths[:dim], count, lengths[dim] // count, *lengths[dim + 1 :])
    return jnp.moveaxis(blocks, dim, 0)


def sum_at_owner(array, axis, dim):
    blocks = cut_along(array, dim, lax.axis_size(axis))
    arrived = lax.all_to_all(blocks, axis, split_axis=0, concat_axis=0, tiled=True)
    return arrived.sum(axis=0)


def sum_in_two_steps(array, axes, dim):
    far, near = axes
    blocks = cut_along(array, dim, lax.axis_size(far))
    nearer = sum_at_owner(blocks, near, dim + 1)
    arrived = lax.all_to_all(nearer, far, split_axis=0, concat_axis=0, tiled=True)
    return arrived.sum(axis=0)


def of_everyone(array, axis):
    everything = copy_for_each(array, axis)
    return jnp.sum(everything, axis=0)


def by_axis(array, axes):
    far, near = axes
    nearer = of_everyone(array, near)
    return of_everyone(nearer, far)


def in_one(arrays, axis):
    line, at, done = (jnp.concatenate([a.reshape(-1) for a in arrays]), 0, [])
    total = by_axis(line, axis)
    for a in arrays:
        done.append(total[at : at + a.size].reshape(a.shape))
        at += a.size
    return tuple(done)


def column_pass(row_side, rows_mass, column_feats):
    columns = column_feats.shape[1]
    block_width = math.gcd(columns, column_block)
    count_blocks = columns // block_width

    def one_block(block_index):
        segment = lax.dynamic_slice_in_dim(column_feats, block_index * block_width, block_width, 1)
        payoff = jnp.einsum("kr,kc->rc", row_side, segment, precision=lax.Precision.HIGHEST)
        moves = jax.nn.sigmoid(intensity * payoff)
        inflow = jnp.dot(rows_mass, moves, precision=lax.Precision.HIGHEST)
        return (inflow, jnp.sum(moves, axis=1))

    inflows, totals = lax.map(one_block, jnp.arange(count_blocks, dtype=jnp.int32))
    return (inflows.reshape(columns), jnp.sum(totals, axis=0))


def on_device(features, initial):
    half_feat = features.shape[0] // 2
    row_feats = gathered_copies(features, "col", 1)
    row_side = jnp.concatenate([row_feats[half_feat:], -row_feats[:half_feat]], axis=0)
    step_rate = 1.0 / NPOL
    weights = initial / one_axis_at_a_time(jnp.sum(initial), ROW_COL)
    column_feats = gathered_by_axis(features, ROW, (0, 1, 2), 1)
    changes = []
    pending = jnp.zeros((), jnp.float32)
    own_totals = jnp.zeros_like(weights)
    for iteration in range(ITERS):
        rows_mass = gathered_copies(weights, "col", 0)
        inflow, totals = column_pass(row_side, rows_mass, column_feats)
        if iteration == 0:
            own_totals = sum_at_owner(totals, "col", 0)
        summed = sum_in_two_steps(inflow, ("row_0", ("row_1", "row_2")), 0)
        advanced = step_rate * summed + weights * (1.0 - step_rate * own_totals)
        normalizer, earlier = in_one(
            (jnp.sum(advanced), pending), ("row_0", ("row_1", "row_2", "col"))
        )
        if iteration > 0:
            changes.append(earlier)
        updated = advanced / normalizer
        pending = jnp.sum(jnp.abs(updated - weights))
        weights = updated
    changes.append(one_axis_at_a_time(pending, ROW_COL))
    return (NPOL * weights, jnp.stack(changes))


def solution(mesh):
    torus = Mesh(
        mesh.devices.reshape(4, 4, 8, mesh.shape["col"]), ("row_0", "row_1", "row_2", "col")
    )
    in_specs = (P(None, ROW_COL), P(ROW_COL))
    out_specs = (P(ROW_COL), P())
    return jax.shard_map(
        on_device, mesh=torus, in_specs=in_specs, out_specs=out_specs, check_vma=False
    )
```

profile of v0, /device:TPU:1, one launch (start us, length us, event | category | flops | bytes accessed | tf_op | source)
XLA Modules:
  0.0 353.5 jit_solution(2726497459547294447)
XLA Ops:
  7.2 10.8 %all-gather = f32[256,128]{1,0:T(8,128)S(1)} all-gather(f32[64,128]{1,0:T(8,128)} %param.6), channel_id=2, replica_groups=mesh['row_0'=4,'row_1'=4,'row_2'=8,'col'=2] {'row_0'}, dimensions={0}, use_global_device_ids=true | all-gather | bytes 163840 | tf_op jit(solution)/shard_map/all_gather | solution.py:39
  18.0 11.0 %all_gather.10 = f32[16,64,128]{2,1,0:T(8,128)} all-gather(f32[4,64,128]{2,1,0:T(8,128)S(1)} %bitcast.79), channel_id=1, replica_groups=mesh['row_0'=4,'row_1'=4,'row_2'=8,'col'=2] {'row_1'}, dimensions={0}, use_global_device_ids=true | all-gather | bytes 655360 | tf_op jit(solution)/shard_map/all_gather | solution.py:39
  30.3 8.7 %psum.56 = f32[]{:T(128)} all-reduce(f32[]{:T(128)} %reduce_sum.144), channel_id=1, replica_groups=mesh['row_0'=4,'row_1'=4,'row_2'=8,'col'=2] {'row_0'}, use_global_device_ids=true, to_apply=%region_1.0 | all-reduce | flops 1 | bytes 8 | tf_op jit(solution)/shard_map/psum | solution.py:33
  39.0 9.2 %psum.57 = f32[]{:T(128)} all-reduce(f32[]{:T(128)} %psum.56), channel_id=1, replica_groups=mesh['row_0'=4,'row_1'=4,'row_2'=8,'col'=2] {'row_1'}, use_global_device_ids=true, to_apply=%region_2.0 | all-reduce | flops 1 | bytes 8 | tf_op jit(solution)/shard_map/psum | solution.py:33
  48.2 19.2 %psum.58 = f32[]{:T(128)} all-reduce(f32[]{:T(128)} %psum.57), channel_id=1, replica_groups=mesh['row_0'=4,'row_1'=4,'row_2'=8,'col'=2] {'row_2'}, use_global_device_ids=true, to_apply=%region_3.0 | all-reduce | flops 1 | bytes 8 | tf_op jit(solution)/shard_map/psum | solution.py:33
  68.8 15.1 %all-to-all-start = ((f32[2,64,128]{2,1,0:T(8,128)}), f32[2,64,128]{2,1,0:T(8,128)S(1)}, u32[]{:S(2)}, u32[]{:S(2)}) async-start(f32[2,64,128]{2,1,0:T(8,128)} %broadcast_in_dim.39), calls=%async_computation | async-start | bytes 131072 | tf_op jit(solution)/shard_map/all_to_all | solution.py:25
  96.9 52.0 %while.22 = (s32[]{:T(128)}, f32[8,2048]{1,0:T(8,128)S(1)}, f32[8,256]{1,0:T(8,128)S(1)}, s32[8]{0:T(128)S(1)}, f32[64,16384]{1,0:T(8,128)}, /*index=5*/f32[64,2...) while((s32[]{:T(128)}, f32[8,2048]{1,0:T(8,128)S(1)}, ...), condition=%wide.region_7.8_spmd, body=%wide.region_5.7_spmd.sunk | while | flops 411565824 | bytes 4812979 | solution.py:102
  149.6 6.0 %all-to-all-start.2 = ((f32[32,4,128]{2,1,0:T(4,128)}), f32[32,4,128]{2,1,0:T(4,128)S(1)}, u32[]{:S(2)}, u32[]{:S(2)}) async-start(f32[32,4,128]{2,1,0:T(4,128)} %copy.25), calls=%async_computation.2 | async-start | bytes 131072 | tf_op jit(solution)/shard_map/all_to_all | solution.py:58
  156.2 8.3 %all-to-all-done.2 = f32[32,4,128]{2,1,0:T(4,128)S(1)} async-done(((f32[32,4,128]{2,1,0:T(4,128)}), f32[32,4,128]{2,1,0:T(4,128)S(1)}, u32[]{:S(2)}, u32[]{:S(2)}) %all-to-all-start.2) | async-done | bytes 65568 | tf_op jit(solution)/shard_map/all_to_all | solution.py:58
  164.5 5.4 %all-to-all-start.4 = ((f32[2,1,128]{2,1,0:T(1,128)}), f32[2,1,128]{2,1,0:T(1,128)S(1)}, u32[]{:S(2)}, u32[]{:S(2)}) async-start(f32[2,1,128]{2,1,0:T(1,128)} %bitcast.18), calls=%async_computation.4 | async-start | bytes 2048 | tf_op jit(solution)/shard_map/all_to_all | solution.py:58
  170.9 4.0 %all-to-all-start.3 = ((f32[4,1,128]{2,1,0:T(1,128)}), f32[4,1,128]{2,1,0:T(1,128)S(1)}, u32[]{:S(2)}, u32[]{:S(2)}) async-start(f32[4,1,128]{2,1,0:T(1,128)} %bitcast.17), calls=%async_computation.3 | async-start | bytes 4096 | tf_op jit(solution)/shard_map/all_to_all | solution.py:66
  181.5 5.9 %all-to-all-start.5 = ((f32[64,1,2]{2,1,0:T(1,128)}), f32[64,1,2]{2,1,0:T(1,128)S(1)}, u32[]{:S(2)}, u32[]{:S(2)}) async-start(f32[64,1,2]{2,1,0:T(1,128)} %broadcast_in_dim.42), calls=%async_computation.5 | async-start | bytes 65536 | tf_op jit(solution)/shard_map/all_to_all | solution.py:25
  187.4 9.4 %all-to-all-done.5 = f32[64,1,2]{2,1,0:T(1,128)S(1)} async-done(((f32[64,1,2]{2,1,0:T(1,128)}), f32[64,1,2]{2,1,0:T(1,128)S(1)}, u32[]{:S(2)}, u32[]{:S(2)}) %all-to-all-start.5) | async-done | bytes 544 | tf_op jit(solution)/shard_map/all_to_all | solution.py:25
  196.9 6.5 %all_to_all.78 = f32[4,1,2]{2,1,0:T(1,128)S(1)} all-to-all(f32[4,1,2]{2,1,0:T(1,128)S(1)} %broadcast_in_dim.43), channel_id=1, replica_groups=mesh['row_0'=4,'row_1'=4,'row_2'=8,'col'=2] {'row_0'}, dimensions={0} | all-to-all | bytes 64 | tf_op jit(solution)/shard_map/all_to_all | solution.py:25
  204.7 5.2 %all_to_all.79 = f32[2,1,128]{2,1,0:T(1,128)S(1)} all-to-all(f32[2,1,128]{2,1,0:T(1,128)S(1)} %broadcast_in_dim.44), channel_id=1, replica_groups=mesh['row_0'=4,'row_1'=4,'row_2'=8,'col'=2] {'col'}, dimensions={0} | all-to-all | bytes 2048 | tf_op jit(solution)/shard_map/all_to_all | solution.py:25
  209.9 51.2 %while.23 = (s32[]{:T(128)}, f32[8,2048]{1,0:T(8,128)S(1)}, s32[8]{0:T(128)S(1)}, f32[64,16384]{1,0:T(8,128)}, f32[64,256]{1,0:T(8,128)S(1)}, /*index=5*/f32[256...) while((s32[]{:T(128)}, f32[8,2048]{1,0:T(8,128)S(1)}, s32[8]{0:T(128)S(1)}, ...), condition=%wide.region_16.17_spmd, body=%wide.region_15.16_spmd.sunk | while | flops 411041792 | bytes 4809895 | solution.py:102
  261.2 11.8 %all_to_all.81 = f32[32,4,128]{2,1,0:T(4,128)S(1)} all-to-all(f32[32,4,128]{2,1,0:T(4,128)S(1)} %copy.29), channel_id=1, replica_groups=mesh['row_0'=4,'row_1'=4,'row_2'=8,'col'=2] {'row_1','row_2'}, dimensions={0} | all-to-all | bytes 131072 | tf_op jit(solution)/shard_map/all_to_all | solution.py:58
  273.1 6.5 %all_to_all.82 = f32[4,1,128]{2,1,0:T(1,128)S(1)} all-to-all(f32[4,1,128]{2,1,0:T(1,128)S(1)} %bitcast.88), channel_id=1, replica_groups=mesh['row_0'=4,'row_1'=4,'row_2'=8,'col'=2] {'row_0'}, dimensions={0} | all-to-all | bytes 4096 | tf_op jit(solution)/shard_map/all_to_all | solution.py:66
  281.6 15.4 %all_to_all.83 = f32[64,1,2]{2,1,0:T(1,128)S(1)} all-to-all(f32[64,1,2]{2,1,0:T(1,128)S(1)} %broadcast_in_dim.45), channel_id=1, replica_groups=mesh['row_0'=4,'row_1'=4,'row_2'=8,'col'=2] {'row_1','row_2','col'}, dimensions={0} | all-to-all | bytes 1024 | tf_op jit(solution)/shard_map/all_to_all | solution.py:25
  297.0 6.5 %all_to_all.80 = f32[4,1,2]{2,1,0:T(1,128)S(1)} all-to-all(f32[4,1,2]{2,1,0:T(1,128)S(1)} %broadcast_in_dim.46), channel_id=1, replica_groups=mesh['row_0'=4,'row_1'=4,'row_2'=8,'col'=2] {'row_0'}, dimensions={0} | all-to-all | bytes 64 | tf_op jit(solution)/shard_map/all_to_all | solution.py:25
  305.4 7.5 %psum.60 = f32[]{:T(128)} all-reduce(f32[]{:T(128)} %get-tuple-element.101), channel_id=1, replica_groups=mesh['row_0'=4,'row_1'=4,'row_2'=8,'col'=2] {'row_0'}, use_global_device_ids=true, to_apply=%region_24.25 | all-reduce | flops 1 | bytes 8 | tf_op jit(solution)/shard_map/psum | solution.py:33
  312.9 7.4 %psum.61 = f32[]{:T(128)} all-reduce(f32[]{:T(128)} %psum.60), channel_id=1, replica_groups=mesh['row_0'=4,'row_1'=4,'row_2'=8,'col'=2] {'row_1'}, use_global_device_ids=true, to_apply=%region_25.26 | all-reduce | flops 1 | bytes 8 | tf_op jit(solution)/shard_map/psum | solution.py:33
  320.3 11.6 %psum.62 = f32[]{:T(128)} all-reduce(f32[]{:T(128)} %psum.61), channel_id=1, replica_groups=mesh['row_0'=4,'row_1'=4,'row_2'=8,'col'=2] {'row_2'}, use_global_device_ids=true, to_apply=%region_26.27 | all-reduce | flops 1 | bytes 8 | tf_op jit(solution)/shard_map/psum | solution.py:33
  331.9 12.3 %psum.63 = f32[1]{0:T(128)} all-reduce(f32[1]{0:T(128)} %bitcast.28), channel_id=1, replica_groups=mesh['row_0'=4,'row_1'=4,'row_2'=8,'col'=2] {'col'}, use_global_device_ids=true, to_apply=%region_27.28 | all-reduce | flops 1 | bytes 8 | tf_op jit(solution)/shard_map/psum | solution.py:33
  (125 shorter events, 125.0 us)
Async XLA Ops:
  7.2 85.0 %all-gather.3.cloned.1.call-start = ((), (), s32[]{:S(2)}) async-start(), calls=%async_computation.12 | async-start | bytes 4718592 | tf_op jit(solution)/shard_map/all_gather | solution.py:39
  68.8 19.5 %all-to-all-start = ((f32[2,64,128]{2,1,0:T(8,128)}), f32[2,64,128]{2,1,0:T(8,128)S(1)}, u32[]{:S(2)}, u32[]{:S(2)}) async-start(f32[2,64,128]{2,1,0:T(8,128)} %broadcast_in_dim.39), calls=%async_computation | async-start | bytes 131072 | tf_op jit(solution)/shard_map/all_to_all | solution.py:25
  88.9 8.0 %all-to-all-start.1 = ((f32[2,1,128]{2,1,0:T(1,128)}), f32[2,1,128]{2,1,0:T(1,128)S(1)}, u32[]{:S(2)}, u32[]{:S(2)}) async-start(f32[2,1,128]{2,1,0:T(1,128)} %broadcast_in_dim.41), calls=%async_computation.1 | async-start | bytes 2048 | tf_op jit(solution)/shard_map/all_to_all | solution.py:25
  96.9 82.0 %copy-start = (f32[128]{0:T(128)S(1)}, f32[128]{0:T(128)}, u32[]{:S(2)}) copy-start(f32[128]{0:T(128)} %param.7) | copy-start | bytes 1540
  149.6 14.9 %all-to-all-start.2 = ((f32[32,4,128]{2,1,0:T(4,128)}), f32[32,4,128]{2,1,0:T(4,128)S(1)}, u32[]{:S(2)}, u32[]{:S(2)}) async-start(f32[32,4,128]{2,1,0:T(4,128)} %copy.25), calls=%async_computation.2 | async-start | bytes 131072 | tf_op jit(solution)/shard_map/all_to_all | solution.py:58
  164.5 6.4 %all-to-all-start.4 = ((f32[2,1,128]{2,1,0:T(1,128)}), f32[2,1,128]{2,1,0:T(1,128)S(1)}, u32[]{:S(2)}, u32[]{:S(2)}) async-start(f32[2,1,128]{2,1,0:T(1,128)} %bitcast.18), calls=%async_computation.4 | async-start | bytes 2048 | tf_op jit(solution)/shard_map/all_to_all | solution.py:58
  170.9 8.0 %all-to-all-start.3 = ((f32[4,1,128]{2,1,0:T(1,128)}), f32[4,1,128]{2,1,0:T(1,128)S(1)}, u32[]{:S(2)}, u32[]{:S(2)}) async-start(f32[4,1,128]{2,1,0:T(1,128)} %bitcast.17), calls=%async_computation.3 | async-start | bytes 4096 | tf_op jit(solution)/shard_map/all_to_all | solution.py:66
  181.5 15.3 %all-to-all-start.5 = ((f32[64,1,2]{2,1,0:T(1,128)}), f32[64,1,2]{2,1,0:T(1,128)S(1)}, u32[]{:S(2)}, u32[]{:S(2)}) async-start(f32[64,1,2]{2,1,0:T(1,128)} %broadcast_in_dim.42), calls=%async_computation.5 | async-start | bytes 65536 | tf_op jit(solution)/shard_map/all_to_all | solution.py:25
Sparse Core Ops, SparseCore 0:
  29.2 62.1 all-gather.2
where the time goes:
time: 355 us; the launch traced here: 353 us
  blocking collectives  153 us (43%)
  matrix products  79.7 us (22%)
  starting transfers between devices  39.7 us (11%)
  waiting for transfers between devices  22.1 us (6%)
  local copies, waits for them, and re-layouts  21.5 us (6%)
  between operations  14.1 us (4%)
  other arithmetic  12.9 us (4%)
  loops' own time  10.7 us (3%)
    psum x8, blocking collectives, one_axis_at_a_time(): return functools.reduce(lax.psum, axes, array)  79 us
    dot_general x16, matrix products, one_block(): jnp.einsum('kr,kc->rc', row_side, segment, precision=lax.Precision.HIGHEST)  50 us
    all_to_all x4, blocking collectives, copy_for_each(): return lax.all_to_all(copies, axis, split_axis=0, concat_axis=0, tiled=True)  33.5 us
    dot_general x16, matrix products, one_block(): inflow = jnp.dot(rows_mass, moves, precision=lax.Precision.HIGHEST)  29.7 us
    all_to_all x3, starting transfers between devices, copy_for_each(): return lax.all_to_all(copies, axis, split_axis=0, concat_axis=0, tiled=True)  24.3 us
    all_gather x2, blocking collectives, all_blocks(): blocks = lax.all_gather(blocks, axes[k], axis=0, tiled=True)  21.8 us
    all_to_all x1, blocking collectives, sum_at_owner(): lax.all_to_all(blocks, axis, split_axis=0, concat_axis=0, tiled=True)  11.8 us
    all_to_all x2, starting transfers between devices, sum_at_owner(): lax.all_to_all(blocks, axis, split_axis=0, concat_axis=0, tiled=True)  11.4 us
  transfers between devices with their start and end apart: 7, of which 4 were waited for; matrix products, arithmetic and copies ran while one was open for 3% of the time, Pallas kernels for 0%

commit v1 on v0

--- a/solution.py
+++ b/solution.py
@@ -12,6 +12,11 @@
 ROW = ("row_0", "row_1", "row_2")
 intensity = 0.25
 column_block = 2048
+
+
+def exchange_gather(block, axis, d):
+    outgoing = jnp.stack([block] * lax.axis_size(axis))
+    return jnp.concatenate(lax.all_to_all(outgoing, axis, 0, 0), axis=d)
 
 
 def in_order(blocks, dim):
@@ -36,7 +41,7 @@
 def all_blocks(array, axes, turns):
     blocks = array[None]
     for k in turns:
-        blocks = lax.all_gather(blocks, axes[k], axis=0, tiled=True)
+        blocks = exchange_gather(blocks, axes[k], 0)
     block = [lax.axis_size(axes[k]) for k in reversed(turns)]
     blocks = blocks.reshape(*block, *array.shape)
     turned = sorted(range(len(turns)), key=lambda place: turns[len(turns) - 1 - place])

time: 355 us -> 405 us (1.14)
  blocking collectives: 153 us -> 222 us
  between operations: 14.1 us -> 0.78 us
  starting transfers between devices: 39.7 us -> 31.8 us
    psum x8, blocking collectives: 79 us -> 145 us  [one_axis_at_a_time(): return functools.reduce(lax.psum, axes, array)]
    all_gather x2 -> x0, blocking collectives: 21.8 us -> none  [all_blocks(): blocks = lax.all_gather(blocks, axes[k], axis=0, tiled=True)]
    all_to_all x0 -> x2, blocking collectives: none -> 18.1 us  [exchange_gather(): return jnp.concatenate(lax.all_to_all(outgoing, axis, 0, 0), axis=d)]
    all_to_all x3 -> x2, starting transfers between devices: 24.3 us -> 9.09 us  [copy_for_each(): return lax.all_to_all(copies, axis, split_axis=0, concat_axis=0, tiled=True)]
    all_to_all x0 -> x1, starting transfers between devices: none -> 8.32 us  [exchange_gather(): return jnp.concatenate(lax.all_to_all(outgoing, axis, 0, 0), axis=d)]
    all_to_all x4 -> x5, blocking collectives: 33.5 us -> 40.1 us  [copy_for_each(): return lax.all_to_all(copies, axis, split_axis=0, concat_axis=0, tiled=True)]
    all_to_all x3 -> x2, waiting for transfers between devices: 9.43 us -> 9.43 us  [copy_for_each(): return lax.all_to_all(copies, axis, split_axis=0, concat_axis=0, tiled=True)]
  transfers between devices with their start and end apart: 7 -> 6, of which waited for: 4 -> 4; matrix products, arithmetic and copies ran while one was open for 3% -> 2% of each run, Pallas kernels for 0% -> 0%
where the time goes in v1:
time: 405 us; the launch traced here: 403 us
  blocking collectives  222 us (55%)
  matrix products  79.7 us (20%)
  starting transfers between devices  31.8 us (8%)
  local copies, waits for them, and re-layouts  24.2 us (6%)
  waiting for transfers between devices  22 us (5%)
  other arithmetic  11.6 us (3%)
  loops' own time  10.7 us (3%)
    psum x8, blocking collectives, one_axis_at_a_time(): return functools.reduce(lax.psum, axes, array)  145 us
    dot_general x16, matrix products, one_block(): jnp.einsum('kr,kc->rc', row_side, segment, precision=lax.Precision.HIGHEST)  50 us
    all_to_all x5, blocking collectives, copy_for_each(): return lax.all_to_all(copies, axis, split_axis=0, concat_axis=0, tiled=True)  40.1 us
    dot_general x16, matrix products, one_block(): inflow = jnp.dot(rows_mass, moves, precision=lax.Precision.HIGHEST)  29.7 us
    all_to_all x2, blocking collectives, exchange_gather(): return jnp.concatenate(lax.all_to_all(outgoing, axis, 0, 0), axis=d)  18.1 us
    all_to_all x1, blocking collectives, sum_at_owner(): lax.all_to_all(blocks, axis, split_axis=0, concat_axis=0, tiled=True)  11.8 us
    all_to_all x2, starting transfers between devices, sum_at_owner(): lax.all_to_all(blocks, axis, split_axis=0, concat_axis=0, tiled=True)  11.2 us
    another operation x2, loops' own time, column_pass(): lax.map(one_block, jnp.arange(count_blocks, dtype=jnp.int32))  10.7 us
  transfers between devices with their start and end apart: 6, of which 4 were waited for; matrix products, arithmetic and copies ran while one was open for 2% of the time, Pallas kernels for 0%

profile of v1, /device:TPU:1, one launch (start us, length us, event | category | flops | bytes accessed | tf_op | source)
XLA Modules:
  0.0 402.8 jit_solution(8859816821359746671)
XLA Ops:
  1.4 6.6 %all_to_all.93 = f32[2,64,128]{2,1,0:T(8,128)S(1)} all-to-all(f32[2,64,128]{2,1,0:T(8,128)S(1)} %broadcast_in_dim.35), channel_id=1, replica_groups=mesh['row_0'=4,'row_1'=4,'row_2'=8,'col'=2] {'col'}, dimensions={0} | all-to-all | bytes 131072 | tf_op jit(solution)/shard_map/all_to_all | solution.py:30
  8.8 7.2 %all_to_all.94 = f32[4,1,64,128]{3,2,1,0:T(8,128)S(1)} all-to-all(f32[4,1,64,128]{3,2,1,0:T(8,128)S(1)} %stack.15), channel_id=1, replica_groups=mesh['row_0'=4,'row_1'=4,'row_2'=8,'col'=2] {'row_0'}, dimensions={0} | all-to-all | bytes 262144 | tf_op jit(solution)/shard_map/all_to_all | solution.py:19
  16.1 10.9 %all_to_all.95 = f32[4,4,64,128]{3,2,1,0:T(8,128)S(1)} all-to-all(f32[4,4,64,128]{3,2,1,0:T(8,128)S(1)} %stack.16), channel_id=1, replica_groups=mesh['row_0'=4,'row_1'=4,'row_2'=8,'col'=2] {'row_1'}, dimensions={0} | all-to-all | bytes 1048576 | tf_op jit(solution)/shard_map/all_to_all | solution.py:19
  29.5 8.3 %all-to-all-start.2 = ((f32[8,16,64,128]{3,2,1,0:T(8,128)}), f32[8,16,64,128]{3,2,1,0:T(8,128)}, u32[]{:S(2)}, u32[]{:S(2)}) async-start(f32[8,16,64,128]{3,2,1,0:T(8,128)} %stack.17), calls=%async_computation.2 | async-start | bytes 8388608 | tf_op jit(solution)/shard_map/all_to_all | solution.py:19
  38.4 7.5 %psum.56 = f32[]{:T(128)} all-reduce(f32[]{:T(128)} %reduce_sum.144), channel_id=1, replica_groups=mesh['row_0'=4,'row_1'=4,'row_2'=8,'col'=2] {'row_0'}, use_global_device_ids=true, to_apply=%region_1.0 | all-reduce | flops 1 | bytes 8 | tf_op jit(solution)/shard_map/psum | solution.py:38
  45.9 8.3 %psum.57 = f32[]{:T(128)} all-reduce(f32[]{:T(128)} %psum.56), channel_id=1, replica_groups=mesh['row_0'=4,'row_1'=4,'row_2'=8,'col'=2] {'row_1'}, use_global_device_ids=true, to_apply=%region_2.0 | all-reduce | flops 1 | bytes 8 | tf_op jit(solution)/shard_map/psum | solution.py:38
  54.2 82.7 %psum.58 = f32[]{:T(128)} all-reduce(f32[]{:T(128)} %psum.57), channel_id=1, replica_groups=mesh['row_0'=4,'row_1'=4,'row_2'=8,'col'=2] {'row_2'}, use_global_device_ids=true, to_apply=%region_3.0 | all-reduce | flops 1 | bytes 8 | tf_op jit(solution)/shard_map/psum | solution.py:38
  136.9 8.0 %psum.59 = f32[]{:T(128)} all-reduce(f32[]{:T(128)} %psum.58), channel_id=1, replica_groups=mesh['row_0'=4,'row_1'=4,'row_2'=8,'col'=2] {'col'}, use_global_device_ids=true, to_apply=%region_4.0 | all-reduce | flops 1 | bytes 8 | tf_op jit(solution)/shard_map/psum | solution.py:38
  154.4 52.0 %while.22 = (s32[]{:T(128)}, f32[8,2048]{1,0:T(8,128)S(1)}, f32[8,256]{1,0:T(8,128)S(1)}, s32[8]{0:T(128)S(1)}, f32[64,16384]{1,0:T(8,128)}, /*index=5*/f32[64,2...) while((s32[]{:T(128)}, f32[8,2048]{1,0:T(8,128)S(1)}, ...), condition=%wide.region_7.8_spmd, body=%wide.region_5.7_spmd.sunk | while | flops 411565824 | bytes 4812979 | solution.py:107
  207.1 6.6 %all-to-all-start.5 = ((f32[32,4,128]{2,1,0:T(4,128)}), f32[32,4,128]{2,1,0:T(4,128)S(1)}, u32[]{:S(2)}, u32[]{:S(2)}) async-start(f32[32,4,128]{2,1,0:T(4,128)} %copy.25), calls=%async_computation.5 | async-start | bytes 131072 | tf_op jit(solution)/shard_map/all_to_all | solution.py:63
  214.3 8.3 %all-to-all-done.5 = f32[32,4,128]{2,1,0:T(4,128)S(1)} async-done(((f32[32,4,128]{2,1,0:T(4,128)}), f32[32,4,128]{2,1,0:T(4,128)S(1)}, u32[]{:S(2)}, u32[]{:S(2)}) %all-to-all-start.5) | async-done | bytes 65568 | tf_op jit(solution)/shard_map/all_to_all | solution.py:63
  237.9 5.6 %all-to-all-start.8 = ((f32[64,1,2]{2,1,0:T(1,128)}), f32[64,1,2]{2,1,0:T(1,128)S(1)}, u32[]{:S(2)}, u32[]{:S(2)}) async-start(f32[64,1,2]{2,1,0:T(1,128)} %broadcast_in_dim.38), calls=%async_computation.8 | async-start | bytes 65536 | tf_op jit(solution)/shard_map/all_to_all | solution.py:30
  243.6 9.4 %all-to-all-done.8 = f32[64,1,2]{2,1,0:T(1,128)S(1)} async-done(((f32[64,1,2]{2,1,0:T(1,128)}), f32[64,1,2]{2,1,0:T(1,128)S(1)}, u32[]{:S(2)}, u32[]{:S(2)}) %all-to-all-start.8) | async-done | bytes 544 | tf_op jit(solution)/shard_map/all_to_all | solution.py:30
  253.1 6.5 %all_to_all.96 = f32[4,1,2]{2,1,0:T(1,128)S(1)} all-to-all(f32[4,1,2]{2,1,0:T(1,128)S(1)} %broadcast_in_dim.39), channel_id=1, replica_groups=mesh['row_0'=4,'row_1'=4,'row_2'=8,'col'=2] {'row_0'}, dimensions={0} | all-to-all | bytes 64 | tf_op jit(solution)/shard_map/all_to_all | solution.py:30
  260.9 5.2 %all_to_all.97 = f32[2,1,128]{2,1,0:T(1,128)S(1)} all-to-all(f32[2,1,128]{2,1,0:T(1,128)S(1)} %broadcast_in_dim.40), channel_id=1, replica_groups=mesh['row_0'=4,'row_1'=4,'row_2'=8,'col'=2] {'col'}, dimensions={0} | all-to-all | bytes 2048 | tf_op jit(solution)/shard_map/all_to_all | solution.py:30
  266.0 51.3 %while.23 = (s32[]{:T(128)}, f32[8,2048]{1,0:T(8,128)S(1)}, s32[8]{0:T(128)S(1)}, f32[64,16384]{1,0:T(8,128)}, f32[64,256]{1,0:T(8,128)S(1)}, /*index=5*/f32[256...) while((s32[]{:T(128)}, f32[8,2048]{1,0:T(8,128)S(1)}, s32[8]{0:T(128)S(1)}, ...), condition=%wide.region_16.17_spmd, body=%wide.region_15.16_spmd.sunk | while | flops 411041792 | bytes 4809895 | solution.py:107
  317.4 11.8 %all_to_all.99 = f32[32,4,128]{2,1,0:T(4,128)S(1)} all-to-all(f32[32,4,128]{2,1,0:T(4,128)S(1)} %copy.29), channel_id=1, replica_groups=mesh['row_0'=4,'row_1'=4,'row_2'=8,'col'=2] {'row_1','row_2'}, dimensions={0} | all-to-all | bytes 131072 | tf_op jit(solution)/shard_map/all_to_all | solution.py:63
  329.2 6.5 %all_to_all.100 = f32[4,1,128]{2,1,0:T(1,128)S(1)} all-to-all(f32[4,1,128]{2,1,0:T(1,128)S(1)} %bitcast.89), channel_id=1, replica_groups=mesh['row_0'=4,'row_1'=4,'row_2'=8,'col'=2] {'row_0'}, dimensions={0} | all-to-all | bytes 4096 | tf_op jit(solution)/shard_map/all_to_all | solution.py:71
  337.7 15.4 %all_to_all.101 = f32[64,1,2]{2,1,0:T(1,128)S(1)} all-to-all(f32[64,1,2]{2,1,0:T(1,128)S(1)} %broadcast_in_dim.41), channel_id=1, replica_groups=mesh['row_0'=4,'row_1'=4,'row_2'=8,'col'=2] {'row_1','row_2','col'}, dimensions={0} | all-to-all | bytes 1024 | tf_op jit(solution)/shard_map/all_to_all | solution.py:30
  353.2 6.5 %all_to_all.98 = f32[4,1,2]{2,1,0:T(1,128)S(1)} all-to-all(f32[4,1,2]{2,1,0:T(1,128)S(1)} %broadcast_in_dim.42), channel_id=1, replica_groups=mesh['row_0'=4,'row_1'=4,'row_2'=8,'col'=2] {'row_0'}, dimensions={0} | all-to-all | bytes 64 | tf_op jit(solution)/shard_map/all_to_all | solution.py:30
  361.6 7.5 %psum.60 = f32[]{:T(128)} all-reduce(f32[]{:T(128)} %get-tuple-element.101), channel_id=1, replica_groups=mesh['row_0'=4,'row_1'=4,'row_2'=8,'col'=2] {'row_0'}, use_global_device_ids=true, to_apply=%region_24.25 | all-reduce | flops 1 | bytes 8 | tf_op jit(solution)/shard_map/psum | solution.py:38
  369.1 7.4 %psum.61 = f32[]{:T(128)} all-reduce(f32[]{:T(128)} %psum.60), channel_id=1, replica_groups=mesh['row_0'=4,'row_1'=4,'row_2'=8,'col'=2] {'row_1'}, use_global_device_ids=true, to_apply=%region_25.26 | all-reduce | flops 1 | bytes 8 | tf_op jit(solution)/shard_map/psum | solution.py:38
  376.4 11.6 %psum.62 = f32[]{:T(128)} all-reduce(f32[]{:T(128)} %psum.61), channel_id=1, replica_groups=mesh['row_0'=4,'row_1'=4,'row_2'=8,'col'=2] {'row_2'}, use_global_device_ids=true, to_apply=%region_26.27 | all-reduce | flops 1 | bytes 8 | tf_op jit(solution)/shard_map/psum | solution.py:38
  388.1 12.3 %psum.63 = f32[1]{0:T(128)} all-reduce(f32[1]{0:T(128)} %bitcast.29), channel_id=1, replica_groups=mesh['row_0'=4,'row_1'=4,'row_2'=8,'col'=2] {'col'}, use_global_device_ids=true, to_apply=%region_27.28 | all-reduce | flops 1 | bytes 8 | tf_op jit(solution)/shard_map/psum | solution.py:38
  (126 shorter events, 131.1 us)
Async XLA Ops:
  29.5 8.3 %copy-start = (f32[128]{0:T(128)S(1)}, f32[128]{0:T(128)}, u32[]{:S(2)}) copy-start(f32[128]{0:T(128)} %param.7) | copy-start | bytes 1540
  29.5 116.1 %all-to-all-start.2 = ((f32[8,16,64,128]{3,2,1,0:T(8,128)}), f32[8,16,64,128]{3,2,1,0:T(8,128)}, u32[]{:S(2)}, u32[]{:S(2)}) async-start(f32[8,16,64,128]{3,2,1,0:T(8,128)} %stack.17), calls=%async_computation.2 | async-start | bytes 8388608 | tf_op jit(solution)/shard_map/all_to_all | solution.py:19
  146.2 8.2 %all-to-all-start.4 = ((f32[2,1,128]{2,1,0:T(1,128)}), f32[2,1,128]{2,1,0:T(1,128)S(1)}, u32[]{:S(2)}, u32[]{:S(2)}) async-start(f32[2,1,128]{2,1,0:T(1,128)} %broadcast_in_dim.37), calls=%async_computation.4 | async-start | bytes 2048 | tf_op jit(solution)/shard_map/all_to_all | solution.py:30
  207.1 15.5 %all-to-all-start.5 = ((f32[32,4,128]{2,1,0:T(4,128)}), f32[32,4,128]{2,1,0:T(4,128)S(1)}, u32[]{:S(2)}, u32[]{:S(2)}) async-start(f32[32,4,128]{2,1,0:T(4,128)} %copy.25), calls=%async_computation.5 | async-start | bytes 131072 | tf_op jit(solution)/shard_map/all_to_all | solution.py:63
  222.6 5.6 %all-to-all-start.7 = ((f32[2,1,128]{2,1,0:T(1,128)}), f32[2,1,128]{2,1,0:T(1,128)S(1)}, u32[]{:S(2)}, u32[]{:S(2)}) async-start(f32[2,1,128]{2,1,0:T(1,128)} %bitcast.19), calls=%async_computation.7 | async-start | bytes 2048 | tf_op jit(solution)/shard_map/all_to_all | solution.py:63
  228.2 7.1 %all-to-all-start.6 = ((f32[4,1,128]{2,1,0:T(1,128)}), f32[4,1,128]{2,1,0:T(1,128)S(1)}, u32[]{:S(2)}, u32[]{:S(2)}) async-start(f32[4,1,128]{2,1,0:T(1,128)} %bitcast.18), calls=%async_computation.6 | async-start | bytes 4096 | tf_op jit(solution)/shard_map/all_to_all | solution.py:71
  237.9 15.1 %all-to-all-start.8 = ((f32[64,1,2]{2,1,0:T(1,128)}), f32[64,1,2]{2,1,0:T(1,128)S(1)}, u32[]{:S(2)}, u32[]{:S(2)}) async-start(f32[64,1,2]{2,1,0:T(1,128)} %broadcast_in_dim.38), calls=%async_computation.8 | async-start | bytes 65536 | tf_op jit(solution)/shard_map/all_to_all | solution.py:30
